TPU v7x, 32 devices: a whole 2x2x4 slice. The times are simulated.
32 devices in a mesh: dp: 2 (over x), tp: 4 (over z), sp: 4 (over y, core).
Axes of the slice: x: 2, y: 2, z: 4, core: 2. Of those that a mesh axis runs over, the one named last changes fastest.
Arguments:
- x_in: bfloat16 [131072, 192], P(('dp', 'sp')), parts along dimension 0
- grad_y: bfloat16 [131072, 192], P(('dp', 'sp')), parts along dimension 0
- w_qkv: bfloat16 [192, 3, 192], P(None, None, 'tp')
- w_out: bfloat16 [192, 192], P('tp')
- ln_gamma: float32 [192], replicated
- ln_beta: float32 [192], replicated
- temperature: float32 [4], replicated
Outputs:
- output 1: bfloat16 [131072, 192], P(('dp', 'sp')), parts along dimension 0
- output 2: bfloat16 [131072, 192], P(('dp', 'sp')), parts along dimension 0
- output 3: float32 [384, 3, 192], P(('dp', 'sp'), None, 'tp'), parts along dimension 0
- output 4: float32 [384, 192], P(('dp', 'tp', 'sp')), parts along dimension 0
- output 5: float32 [384], P('dp'), parts along dimension 0
- output 6: float32 [384], P('dp'), parts along dimension 0
- output 7: float32 [8], P('dp'), parts along dimension 0
There are 2 independent parts. A program takes and returns all parts, laid end to end along the dimension named above; an argument that names none is the same for every part.
All inputs are finite; a program needn't handle non-finite values.
Results may differ from a plain program's by a relative error of at most 0.001.
Values are sent between devices in bfloat16 or wider.
A program may use at most 1 GiB of HBM per device.

v0:
```python
import jax
import jax.numpy as jnp
from jax import lax
from jax.sharding import PartitionSpec as P

LN_EPS = 1e-6


def layer_norm_fwd(x_rows, ln_gamma, ln_beta):
    x_float = x_rows.astype(jnp.float32)
    centered = x_float - jnp.mean(x_float, axis=-1, keepdims=True)
    inv_std = lax.rsqrt(jnp.mean(centered * centered, axis=-1, keepdims=True) + LN_EPS)
    x_hat = centered * inv_std
    return x_hat, inv_std, (x_hat * ln_gamma + ln_beta).astype(jnp.bfloat16)


def layer_norm_bwd(grad_u, x_hat, inv_std, ln_gamma):
    value_a9 = grad_u * ln_gamma
    return inv_std * (value_a9 - jnp.mean(value_a9, axis=-1, keepdims=True) - x_hat * jnp.mean(value_a9 * x_hat, axis=-1, keepdims=True))


def state_forward(gram_mat, q_sq, k_sq, temp_heads):
    norm_prod = jnp.sqrt(q_sq)[:, :, None] * jnp.sqrt(k_sq)[:, None, :]
    gram_n = gram_mat / norm_prod
    attn_prob = jax.nn.softmax(temp_heads[:, None, None] * gram_n, axis=-1)
    return gram_n, norm_prod, attn_prob


def state_backward(d_attn, attn_prob, gram_n, norm_prod, q_sq, k_sq, temp_heads):
    d_logit = attn_prob * (d_attn - jnp.sum(attn_prob * d_attn, axis=-1, keepdims=True))
    temp_grad = jnp.sum(d_logit * gram_n, axis=(1, 2))
    grad_sn = temp_heads[:, None, None] * d_logit
    d_gram = (grad_sn / norm_prod).astype(jnp.bfloat16)
    prod_sn = grad_sn * gram_n
    q_coef = -jnp.sum(prod_sn, axis=2) / q_sq
    k_coef = -jnp.sum(prod_sn, axis=1) / k_sq
    return d_gram, q_coef, k_coef, temp_grad


def solution(mesh):
    tp_size = mesh.shape["tp"]
    row_spec = P(("dp", "sp"), None)

    def local_step(x_blk, grad_blk, w_qkv, w_out, ln_gamma, ln_beta, value_a11):
        tokens, model_width = x_blk.shape
        local_cols = w_qkv.shape[2]
        heads_loc = value_a11.shape[0] // tp_size
        head_dim = local_cols // heads_loc
        temp_heads = lax.dynamic_slice_in_dim(value_a11, lax.axis_index("tp") * heads_loc, heads_loc)
        x_hat, inv_std, u_act = layer_norm_fwd(x_blk, ln_gamma, ln_beta)
        qkv_act = jnp.einsum("nd,dec->nec", u_act, w_qkv, preferred_element_type=jnp.float32).astype(jnp.bfloat16)
        qkv_heads = qkv_act.reshape(tokens, 3, heads_loc, head_dim)
        q_act = qkv_heads[:, 0]
        k_act = qkv_heads[:, 1]
        v_act = qkv_heads[:, 2]
        gram_part = jnp.einsum("nhi,nhj->hij", q_act, k_act, preferred_element_type=jnp.float32)
        q_part = jnp.einsum("nhi,nhi->hi", q_act, q_act, preferred_element_type=jnp.float32)
        k_part = jnp.einsum("nhj,nhj->hj", k_act, k_act, preferred_element_type=jnp.float32)
        gram_mat, q_sq, k_sq = lax.psum((gram_part, q_part, k_part), "sp")
        gram_n, norm_prod, attn_prob = state_forward(gram_mat, q_sq, k_sq, temp_heads)
        attn_bf = attn_prob.astype(jnp.bfloat16)
        out_act = jnp.einsum("hij,nhj->nhi", attn_bf, v_act, preferred_element_type=jnp.float32).astype(jnp.bfloat16)
        w_out_heads = w_out.reshape(heads_loc, head_dim, model_width)
        y_part = jnp.einsum("nhi,hid->nd", out_act, w_out_heads, preferred_element_type=jnp.float32)
        y_out = (x_blk.astype(jnp.float32) + lax.psum(y_part, "tp")).astype(jnp.bfloat16)
        wout_part = jnp.einsum("nhi,nd->hid", out_act, grad_blk, preferred_element_type=jnp.float32).reshape(local_cols, model_width)
        grad_wout = lax.psum_scatter(wout_part, "sp", scatter_dimension=0, tiled=True)
        dout_act = jnp.einsum("nd,hid->nhi", grad_blk, w_out_heads, preferred_element_type=jnp.float32).astype(jnp.bfloat16)
        d_attn = lax.psum(jnp.einsum("nhi,nhj->hij", dout_act, v_act, preferred_element_type=jnp.float32), "sp")
        dv_act = jnp.einsum("hij,nhi->nhj", attn_bf, dout_act, preferred_element_type=jnp.float32).astype(jnp.bfloat16)
        d_gram, q_coef, k_coef, temp_grad = state_backward(d_attn, attn_prob, gram_n, norm_prod, q_sq, k_sq, temp_heads)
        dq_act = (jnp.einsum("hij,nhj->nhi", d_gram, k_act, preferred_element_type=jnp.float32) + q_act * q_coef).astype(jnp.bfloat16)
        dk_act = (jnp.einsum("hij,nhi->nhj", d_gram, q_act, preferred_element_type=jnp.float32) + k_act * k_coef).astype(jnp.bfloat16)
        dqkv_act = jnp.stack([dq_act, dk_act, dv_act], axis=1).reshape(tokens, 3, local_cols)
        wqkv_part = jnp.einsum("nd,nec->dec", u_act, dqkv_act, preferred_element_type=jnp.float32)
        grad_wqkv = lax.psum_scatter(wqkv_part, "sp", scatter_dimension=0, tiled=True)
        grad_u = lax.psum(jnp.einsum("nec,dec->nd", dqkv_act, w_qkv, preferred_element_type=jnp.float32), "tp")
        grad_gamma, grad_beta = lax.psum((jnp.sum(grad_u * x_hat, axis=0), jnp.sum(grad_u, axis=0)), "sp")
        grad_x = (grad_blk.astype(jnp.float32) + layer_norm_bwd(grad_u, x_hat, inv_std, ln_gamma)).astype(jnp.bfloat16)
        grad_temp = lax.all_gather(temp_grad, "tp", tiled=True)
        return y_out, grad_x, grad_wqkv, grad_wout, grad_gamma, grad_beta, grad_temp

    in_specs = (row_spec, row_spec, P(None, None, "tp"), P("tp", None), P(None), P(None), P(None))
    out_specs = (row_spec, row_spec, P(("dp", "sp"), None, "tp"), P(("dp", "tp", "sp"), None), P("dp"), P("dp"), P("dp"))
    return jax.shard_map(local_step, mesh=mesh, in_specs=in_specs, out_specs=out_specs, check_vma=False)
```

profile of v0, /device:TPU:0, one launch (start us, length us, event | category | flops | bytes accessed | tf_op | source)
XLA Modules:
  0.0 946.5 jit_solution(15571597751154869839)
XLA Ops:
  8.1 3.9 convert_reduce_fusion
  12.1 0.6 copy-done.2
  12.7 1.7 fusion.20
  14.5 5.4 fusion.62
  19.9 4.9 convert_bitcast_fusion
  24.8 0.8 fusion.24
  25.5 1.4 copy-done.4
  26.9 1.6 copy-done.5
  29.1 4.0 convolution_convert_fusion
  33.1 2.0 fusion.32
  35.0 13.5 %all-reduce.4 = (f32[1,48,48]{2,1,0:T(8,128)S(1)}, f32[1,48]{1,0:T(1,128)S(1)}, f32[1,48]{1,0:T(1,128)S(1)}, f32[1,48,48]{2,1,0:T(8,128)S(1)}) all-reduce(f32[1,48,48]{2,1,0:T(8,128)S(1)} %fusion.33, f32[1,48]{1,0:T(1,128)S(1)} %bitcast.104, f32[1,48]{1,0:T(1,128)S(1)} %bitcast.105, ...), channel_id=1, replica_groups=mesh['dp'=2,'tp'=4,'sp'=4] {'sp'}, use_global_device_ids=true, to_apply=%region_2.0 | all-reduce | flops 4704 | bytes 37632 | tf_op jit(solution)/shard_map/psum | solution.py:59
  49.1 0.8 multiply_reduce_fusion.3
  50.0 0.8 fusion.44
  50.8 1.3 fusion.3
  52.2 2.7 convolution_convert_fusion.1
  54.9 0.8 multiply_reduce_fusion.2
  55.7 1.3 multiply_reduce_fusion.1
  57.1 3.2 fusion.4
  60.3 3.3 fusion.5
  63.5 6.4 fusion.64
  70.0 5.5 convolution_bitcast_fusion
  75.5 4.9 fusion.65
  80.5 7.1 fusion
  87.6 1.3 collective-permute-start
  88.9 7.9 fusion.22
  97.5 1.4 dynamic-update-slice
  98.9 13.4 %all-reduce = f32[4]{0:T(128)} all-reduce(f32[4]{0:T(128)S(1)} %dynamic-update-slice), channel_id=1, replica_groups=mesh['dp'=2,'tp'=4,'sp'=4] {'tp'}, use_global_device_ids=true, to_apply=%add | all-reduce | flops 4 | bytes 32
  113.7 0.6 constant_dynamic-slice_fusion
  114.3 791.2 %all-reduce.8.cloned.1.call-done = (f32[16384,192]{0,1:T(8,128)}, f32[16384,192]{0,1:T(8,128)}) async-done(((f32[16384,192]{0,1:T(8,128)}, f32[16384,192]{0,1:T(8,128)}), (f32[16384,192]{0,1:T(8,128)}, f32[16384,192]{0,1:T(8,128)})) %all-reduce.8.cloned.1.call-update) | async-done | bytes 25165840 | tf_op jit(solution)/shard_map/psum | solution.py:65
  905.5 11.2 %fusion.19 = (f32[192]{0:T(256)S(1)}, f32[16384]{0:T(1024)S(1)}, f32[16384]{0:T(1024)S(1)}, f32[192]{0:T(256)S(1)}) fusion(f32[16384,192]{0,1:T(8,128)} %get-tuple-element.21, bf16[16384,192]{0,1:T(8,128)(2,1)} %param.7, f32[16384]{0:T(1024)S(1)} %add_rsqrt_fusion, f32[16384]{0:T(1024)S(1)} %broadcast_multiply_fusion.2, f32[192]{0:T(256)S(1)} %copy-done.8), kind=kLoop, calls=%fused_computation.27 | loop fusion | flops 31424128 | bytes 19138816 | tf_op jit(solution)/shard_map/reduce_sum | solution.py:78
  916.7 15.5 %fusion.18 = (bf16[16384,192]{0,1:T(8,128)(2,1)}, bf16[16384,192]{0,1:T(8,128)(2,1)}) fusion(bf16[16384,192]{0,1:T(8,128)(2,1)} %param.7, bf16[16384,192]{0,1:T(8,128)(2,1)} %param.8, f32[16384,192]{0,1:T(8,128)S(1)} %copy-done.3, f32[16384]{0:T(1024)S(1)} %broadcast_multiply_fusion, f32[16384]{0:T(1024)S(1)} %broadcast_multiply_fusion.1, ...), kind=kLoop, calls=%fused_computation.26 | loop fusion | flops 40894464 | bytes 50594560 | tf_op jit(solution)/shard_map/convert_element_type | solution.py:79
  932.3 6.7 all-reduce.3
  (46 shorter events, 2.7 us)
Async XLA Ops:
  8.0 6.4 copy-start
  8.0 897.5 %all-reduce.8.cloned.1.call-start = ((), (), s32[]{:S(2)}) async-start(), calls=%async_computation.2 | async-start | bytes 50331648 | tf_op jit(solution)/shard_map/psum | solution.py:65
  8.1 4.6 copy-start.2
  12.0 2.4 copy-start.8
  12.0 2.4 copy-start.10
  24.7 2.2 copy-start.4
  24.7 3.7 copy-start.5
  24.8 4.3 copy-start.7
  29.1 19.5 %copy-start.11 = (f32[4]{0:T(128)S(1)}, f32[4]{0:T(128)}, u32[]{:S(2)}) copy-start(f32[4]{0:T(128)} %param.13) | copy-start | bytes 52
  60.2 9.7 %copy-start.6 = (bf16[16384,1,1,48]{0,3,2,1:T(8,128)(2,1)}, bf16[16384,1,1,48]{0,3,2,1:T(8,128)(2,1)S(1)}, u32[]{:S(2)}) copy-start(bf16[16384,1,1,48]{0,3,2,1:T(8,128)(2,1)S(1)} %fusion.4) | copy-start | bytes 4718596
  63.5 6.4 copy-start.13
  75.5 863.5 %reduce-scatter.4.cloned.1.call-start = ((), (), s32[]{:S(2)}) async-start(), calls=%async_computation.1 | async-start | bytes 368640 | tf_op jit(solution)/shard_map/reduce_scatter | solution.py:76
  87.6 9.3 copy-start.12
  87.6 24.7 %copy-start.9 = (u32[32]{0:T(128)S(1)}, u32[32]{0:T(128)}, u32[]{:S(2)}) copy-start(u32[32]{0:T(128)} %constant.32) | copy-start | bytes 388
  87.6 25.9 %collective-permute-start = (f32[12,192]{1,0:T(8,128)S(1)}, f32[12,192]{1,0:T(8,128)S(1)}, u32[]{:S(2)}, u32[]{:S(2)}) collective-permute-start(f32[12,192]{1,0:T(8,128)S(1)} %slice.15), channel_id=1, source_target_pairs={{0,1},{1,2},{2,3},{4,5},{5,6},{6,7},{8,9},{9,10},{10,11},{12,13},{... | collective-permute-start | bytes 27656
  905.5 11.2 %copy-start.3 = (f32[16384,192]{0,1:T(8,128)S(1)}, f32[16384,192]{0,1:T(8,128)}, u32[]{:S(2)}) copy-start(f32[16384,192]{0,1:T(8,128)} %get-tuple-element.21) | copy-start | bytes 37748740
  916.7 22.3 %copy-start.1 = (bf16[192,3,48]{0,2,1:T(8,128)(2,1)S(1)}, bf16[192,3,48]{0,2,1:T(8,128)(2,1)}, u32[]{:S(2)}) copy-start(bf16[192,3,48]{0,2,1:T(8,128)(2,1)} %param.9) | copy-start | bytes 165892
Sparse Core Ops, SparseCore 0:
  75.6 829.8 all-reduce.7
Sparse Core Ops, SparseCore 1:
  99.0 22.2 reduce-scatter.3
where the time goes:
time: 947 us; the launch traced here: 946 us
  waiting for transfers between devices  791 us (84%)
  matrix products  47.1 us (5%)
  other arithmetic  41.9 us (4%)
  blocking collectives  40.8 us (4%)
  between operations  16.5 us (2%)
    psum x1, waiting for transfers between devices, local_step(): lax.psum(y_part, 'tp')  791 us
    unnamed x2, blocking collectives  20.5 us
  transfers between devices with their start and end apart: 3, of which 1 were waited for; matrix products, arithmetic and copies ran while one was open for 5% of the time, Pallas kernels for 0%

commit v1 on v0

v1 whole, which is shorter than its diff:
```python
import jax
import jax.numpy as jnp
from jax import lax
from jax.experimental import pallas as pl
from jax.experimental.pallas import tpu as pltpu
from jax.sharding import PartitionSpec as P

LN_EPS = 1e-6
D = 192
NH = 4
HD = 48
F32 = jnp.float32
BF16 = jnp.bfloat16
MESH = pl.DeviceIdType.MESH
BLK1 = 2048
BLK2 = 2048
SUB = 1024


def dot_nn(a, b):
    return lax.dot_general(a, b, (((1,), (0,)), ((), ())), preferred_element_type=F32)


def dot_nt(a, b):
    return lax.dot_general(a, b, (((1,), (1,)), ((), ())), preferred_element_type=F32)


def norm_cols(x_cols):
    xf = x_cols.astype(F32)
    cen = xf - jnp.sum(xf, axis=0, keepdims=True) * (1.0 / D)
    inv = lax.rsqrt(jnp.sum(cen * cen, axis=0, keepdims=True) * (1.0 / D) + LN_EPS)
    return xf, cen * inv, inv


def fold_lanes(val):
    out = val[:, 0:128]
    for c in range(128, val.shape[1], 128):
        out = out + val[:, c:c + 128]
    return out


def lane_iota(shape):
    return lax.broadcasted_iota(jnp.int32, shape, len(shape) - 1)


def enter(axis, me):
    barrier = pltpu.get_barrier_semaphore()
    for d in range(1, 4):
        pl.semaphore_signal(barrier, inc=1, device_id={axis: lax.rem(me + d, 4)}, device_id_type=MESH)


def remote(src, dst, sems, d, axis, peer):
    return pltpu.make_async_remote_copy(
        src_ref=src, dst_ref=dst, send_sem=sems[0].at[d - 1], recv_sem=sems[1].at[d - 1],
        device_id={axis: peer}, device_id_type=MESH)


def pad_lanes(val, lanes):
    return jnp.concatenate([val, jnp.zeros((val.shape[0], lanes - val.shape[1]), val.dtype)], axis=1)


def pad_rows(val, rows):
    return jnp.concatenate([val, jnp.zeros((rows - val.shape[0], val.shape[1]), val.dtype)], axis=0)


def as_column(row_1d):
    row = jnp.broadcast_to(row_1d.reshape(1, D), (128, D))
    return row.T


def state_kernel(x_hbm, g_hbm, wqkv_ref, wo_ref, gam_ref, bet_ref, temp_ref,
                 wt_out, w_out, mats_ref, vecs_ref, temp_out,
                 xs, gs, wbuf, gram_acc, da_acc, sq_acc, pay_buf, st_send, st_buf, vec_send, vec_buf,
                 in_sems, w_ssem, w_rsem, o_ssem, o_rsem, p_ssem, p_rsem, s_ssem, s_rsem, v_ssem, v_rsem):
    t = lax.axis_index("tp")
    s = lax.axis_index("sp")
    n_load = xs.shape[1] // BLK1

    def loads(c):
        cols = pl.ds(pl.multiple_of(c * BLK1, BLK1), BLK1)
        return (pltpu.make_async_copy(x_hbm.at[:, cols], xs.at[:, cols], in_sems.at[0, c]),
                pltpu.make_async_copy(g_hbm.at[:, cols], gs.at[:, cols], in_sems.at[1, c]))

    for c in range(n_load):
        for cp in loads(c):
            cp.start()
    enter("tp", t)
    enter("sp", s)
    pl.semaphore_wait(pltpu.get_barrier_semaphore(), 6)

    def w_copies(d):
        peer = lax.rem(t + d, 4)
        return (remote(wqkv_ref, wbuf.at[t, pl.ds(0, 3)], (w_ssem, w_rsem), d, "tp", peer),
                remote(wo_ref, wbuf.at[t, 3], (o_ssem, o_rsem), d, "tp", peer))

    for d in range(1, 4):
        for cp in w_copies(d):
            cp.start()
    wbuf[pl.ds(t, 1), 0:3] = wqkv_ref[...][None]
    wbuf[pl.ds(t, 1), 3] = wo_ref[...][None]
    gram_acc[...] = jnp.zeros_like(gram_acc)
    da_acc[...] = jnp.zeros_like(da_acc)
    sq_acc[...] = jnp.zeros_like(sq_acc)
    vecs_ref[2] = as_column(gam_ref[...])
    vecs_ref[3] = as_column(bet_ref[...])
    gamma = vecs_ref[2, :, 0:1]
    beta = vecs_ref[3, :, 0:1]
    w_own = wqkv_ref[...].reshape(3 * HD, D)

    def body(c, carry):
        for cp in loads(c):
            cp.wait()
        cols = pl.ds(pl.multiple_of(c * BLK1, BLK1), BLK1)
        _, xh, _ = norm_cols(xs[:, cols])
        u = (xh * gamma + beta).astype(BF16)
        qkv = dot_nn(w_own, u).astype(BF16)
        do = dot_nn(wo_ref[...], gs[:, cols]).astype(BF16)
        q, k, v = qkv[0:HD], qkv[HD:2 * HD], qkv[2 * HD:3 * HD]
        gram_acc[...] += dot_nt(q, k)
        da_acc[...] += dot_nt(do, v)
        qf = q.astype(F32)
        kf = k.astype(F32)
        sq_acc[0] += fold_lanes(qf * qf)
        sq_acc[1] += fold_lanes(kf * kf)
        return carry

    lax.fori_loop(0, n_load, body, 0)

    lane = lane_iota((HD, 128))
    msg = jnp.where(lane < 64, pad_lanes(gram_acc[...], 128), pltpu.roll(pad_lanes(da_acc[...], 128), 64, 1))
    asq = jnp.sum(sq_acc[0], axis=1, keepdims=True)
    bsq = jnp.sum(sq_acc[1], axis=1, keepdims=True)
    msg = jnp.where(lane == 112, asq, jnp.where(lane == 113, bsq, msg))
    pay_buf[pl.ds(s, 1)] = msg[None]

    def p_copy(d):
        return remote(pay_buf.at[s], pay_buf.at[s], (p_ssem, p_rsem), d, "sp", lax.rem(s + d, 4))

    for d in range(1, 4):
        p_copy(d).start()
    for d in range(1, 4):
        for cp in w_copies(d):
            cp.wait()
    for e in range(4):
        wt_full = wbuf[:, e].reshape(D, D)
        wt_out[e * D:(e + 1) * D] = wt_full
        w_out[e] = wt_full.T
    for d in range(1, 4):
        p_copy(d).wait()

    tot = (pay_buf[0] + pay_buf[1]) + (pay_buf[2] + pay_buf[3])
    row = lax.broadcasted_iota(jnp.int32, (HD, 128), 0)
    live = lane < HD
    eye = lane == row
    temp = temp_ref[t]
    gm = jnp.where(live, tot, 0.0)
    da = jnp.where(live, pltpu.roll(tot, 64, 1), 0.0)
    a_col = tot[:, 112:113]
    b_col = tot[:, 113:114]
    b_row = jnp.sum(jnp.where(eye, b_col, 0.0), axis=0, keepdims=True)
    b_row = jnp.where(lane_iota((1, 128)) < HD, b_row, 1.0)
    norm = jnp.sqrt(a_col) * jnp.sqrt(b_row)
    sn = gm / norm
    logit = jnp.where(live, temp * sn, -1e30)
    ex = jnp.where(live, jnp.exp(logit - jnp.max(logit, axis=1, keepdims=True)), 0.0)
    attn = ex / jnp.sum(ex, axis=1, keepdims=True)
    dl = attn * (da - jnp.sum(attn * da, axis=1, keepdims=True))
    dtau = jnp.sum(jnp.sum(dl * sn, axis=1, keepdims=True), axis=0, keepdims=True)
    grad_sn = temp * dl
    dg = grad_sn / norm
    prod = grad_sn * sn
    cq_col = -jnp.sum(prod, axis=1, keepdims=True) / a_col
    ck_row = -jnp.sum(prod, axis=0, keepdims=True) / b_row
    cq_row = jnp.sum(jnp.where(eye, cq_col, 0.0), axis=0, keepdims=True)
    row8 = lax.broadcasted_iota(jnp.int32, (8, 128), 0)
    vec_send[...] = jnp.where(row8 == 0, cq_row, jnp.where(row8 == 1, ck_row, jnp.where(row8 == 2, dtau, 0.0)))
    for half, val in enumerate((attn, dg)):
        flip = pltpu.roll(pad_rows(val, 128).T[0:HD], 64, 1)
        st_send[:, 128 * half:128 * half + 128] = jnp.where(lane < 64, val, flip).astype(BF16)

    def s_copies(d):
        peer = lax.rem(t + d, 4)
        return (remote(st_send, st_buf.at[t], (s_ssem, s_rsem), d, "tp", peer),
                remote(vec_send, vec_buf.at[t], (v_ssem, v_rsem), d, "tp", peer))

    for d in range(1, 4):
        for cp in s_copies(d):
            cp.start()
    st_buf[pl.ds(t, 1)] = st_send[...][None]
    vec_buf[pl.ds(t, 1)] = vec_send[...][None]
    for d in range(1, 4):
        for cp in s_copies(d):
            cp.wait()
    lane2 = lane_iota((HD, 256))
    vec_t = pad_rows(vec_buf[...].reshape(32, 128), 128).T
    for h in range(NH):
        wide = st_buf[h].astype(F32)
        here = (lane2 >= HD * h) & (lane2 < HD * h + HD)
        for j in range(4):
            shift = (HD * h - 64 * j) % 256
            moved = pltpu.roll(wide, shift, 1) if shift else wide
            mats_ref[j, HD * h:HD * h + HD] = jnp.where(here, moved, 0.0)[:, :D].astype(BF16)
        for j in range(2):
            vecs_ref[j, HD * h:HD * h + HD] = jnp.broadcast_to(vec_t[0:HD, 8 * h + j:8 * h + j + 1], (HD, 128))
    lane8 = lane_iota((8, 128))
    taus = jnp.zeros((8, 128), F32)
    for h in range(NH):
        taus = jnp.where(lane8 == h, vec_buf[h, 2:3, 0:1], taus)
    temp_out[...] = taus


def col_pass(xb, gb, wt_ref, w_ref, mats_ref, vecs_ref):
    cq, ck, gamma, beta = [vecs_ref[j, :, 0:1] for j in range(4)]
    xf, xh, inv = norm_cols(xb)
    u = (xh * gamma + beta).astype(BF16)
    q = dot_nn(wt_ref[0:D], u).astype(BF16)
    k = dot_nn(wt_ref[D:2 * D], u).astype(BF16)
    v = dot_nn(wt_ref[2 * D:3 * D], u).astype(BF16)
    do = dot_nn(wt_ref[3 * D:4 * D], gb).astype(BF16)
    o = dot_nn(mats_ref[0], v).astype(BF16)
    y = (xf + dot_nn(w_ref[3], o)).astype(BF16)
    dv = dot_nn(mats_ref[1], do).astype(BF16)
    dq = (dot_nn(mats_ref[2], k) + q.astype(F32) * cq).astype(BF16)
    dk = (dot_nn(mats_ref[3], q) + k.astype(F32) * ck).astype(BF16)
    du = dot_nn(w_ref[0], dq) + dot_nn(w_ref[1], dk) + dot_nn(w_ref[2], dv)
    gx = du * gamma
    m1 = jnp.sum(gx, axis=0, keepdims=True) * (1.0 / D)
    m2 = jnp.sum(gx * xh, axis=0, keepdims=True) * (1.0 / D)
    dx = (gb.astype(F32) + inv * (gx - m1 - xh * m2)).astype(BF16)
    return y, dx, xh, u, o, du, (dq, dk, dv)


def rows_kernel(tp_ref, x_ref, g_ref, wt_ref, w_ref, mats_ref, vecs_ref, y_ref, dx_ref, send_ref,
                acc_w, acc_v, r_s):
    i = pl.program_id(0)
    own = pl.ds(pl.multiple_of(tp_ref[0] * HD, 16), HD)

    @pl.when(i == 0)
    def _():
        acc_w[...] = jnp.zeros_like(acc_w)
        acc_v[...] = jnp.zeros_like(acc_v)

    for lo in range(0, BLK2, SUB):
        sub = slice(lo, lo + SUB)
        gb = g_ref[:, sub]
        y, dx, xh, u, o, du, r = col_pass(x_ref[:, sub], gb, wt_ref, w_ref, mats_ref, vecs_ref)
        y_ref[:, sub] = y
        dx_ref[:, sub] = dx
        for e in range(3):
            r_s[e] = r[e]
        r_s[3] = o
        acc_w[0:3 * HD] += dot_nt(r_s[0:3, own].reshape(3 * HD, SUB), u)
        acc_w[3 * HD:4 * HD] += dot_nt(r_s[3, own], gb)
        acc_v[0] += fold_lanes(du * xh)
        acc_v[1] += fold_lanes(du)

    @pl.when(i == pl.num_programs(0) - 1)
    def _():
        lane = lane_iota((D, 128))
        dgam = jnp.sum(acc_v[0], axis=1, keepdims=True)
        dbet = jnp.sum(acc_v[1], axis=1, keepdims=True)
        both = jnp.where(lane == 0, dgam, jnp.where(lane == 1, dbet, 0.0))
        dvec = pad_lanes(both.T[0:8], 256)
        wide = [pad_lanes(acc_w[e * HD:(e + 1) * HD], 256) for e in range(4)]
        lane2 = lane_iota((HD, 256))
        for sp in range(4):
            cut = [pltpu.roll(wide[e], (256 + 64 * e - HD * sp) % 256, 1) if 64 * e != HD * sp else wide[e]
                   for e in range(3)]
            msg = jnp.where(lane2 < 64, cut[0], jnp.where(lane2 < 128, cut[1], cut[2]))
            send_ref[sp, 0:HD] = msg
            moved = pltpu.roll(wide[3], HD - 12 * sp, 0) if sp else wide[3]
            send_ref[sp, HD:HD + 16] = moved[0:16]
            send_ref[sp, HD + 16:HD + 24] = dvec


def reduce_kernel(send_ref, out_ref, recv, ssem, rsem):
    s = lax.axis_index("sp")
    enter("sp", s)
    pl.semaphore_wait(pltpu.get_barrier_semaphore(), 3)

    def copy(d):
        peer = lax.rem(s + d, 4)
        return remote(send_ref.at[peer], recv.at[s], (ssem, rsem), d, "sp", peer)

    for d in range(1, 4):
        copy(d).start()
    recv[pl.ds(s, 1)] = send_ref[pl.ds(s, 1)]
    for d in range(1, 4):
        copy(d).wait()
    out_ref[...] = (recv[0] + recv[1]) + (recv[2] + recv[3])


def finish_kernel(res_ref, tau_ref, gw_ref, gwo_ref, gg_ref, gb_ref, gt_ref):
    full = pad_rows(res_ref[0:HD], 128)
    both = full[:, 0:128].T
    gw_ref[0] = both[0:HD, 0:HD]
    gw_ref[1] = both[64:64 + HD, 0:HD]
    gw_ref[2] = full[:, 128:256].T[0:HD, 0:HD]
    gwo_ref[...] = res_ref[HD:HD + 12, 0:D]
    gg_ref[...] = res_ref[HD + 16, 0:D]
    gb_ref[...] = res_ref[HD + 17, 0:D]
    gt_ref[...] = tau_ref[0, 0:NH]


def solution(mesh):
    row_spec = P(("dp", "sp"), None)

    def local_step(x_blk, grad_blk, w_qkv, w_out, ln_gamma, ln_beta, temperature):
        tokens = x_blk.shape[0]
        x_t = x_blk.T
        g_t = grad_blk.T
        wqkv_t = jnp.transpose(w_qkv, (1, 2, 0))
        vmem = pl.BlockSpec(memory_space=pltpu.VMEM)
        hbm = pl.BlockSpec(memory_space=pl.ANY)
        dma = pltpu.SemaphoreType.DMA
        sds = jax.ShapeDtypeStruct
        wt_full, w_full, mats, vecs, taus = pl.pallas_call(
            state_kernel,
            name="state_kernel",
            out_shape=(sds((4 * D, D), BF16), sds((4, D, D), BF16), sds((4, D, D), BF16), sds((4, D, 128), F32),
                       sds((8, 128), F32)),
            in_specs=[hbm, hbm, vmem, vmem, vmem, vmem, pl.BlockSpec(memory_space=pltpu.SMEM)],
            out_specs=(vmem,) * 5,
            scratch_shapes=[
                pltpu.VMEM((D, tokens), BF16), pltpu.VMEM((D, tokens), BF16),
                pltpu.VMEM((4, 4, HD, D), BF16),
                pltpu.VMEM((HD, HD), F32), pltpu.VMEM((HD, HD), F32), pltpu.VMEM((2, HD, 128), F32),
                pltpu.VMEM((4, HD, 128), F32), pltpu.VMEM((HD, 256), BF16), pltpu.VMEM((4, HD, 256), BF16),
                pltpu.VMEM((8, 128), F32), pltpu.VMEM((4, 8, 128), F32),
                dma((2, tokens // BLK1)), dma((3,)), dma((3,)), dma((3,)), dma((3,)), dma((3,)), dma((3,)),
                dma((3,)), dma((3,)), dma((3,)), dma((3,)),
            ],
            compiler_params=pltpu.CompilerParams(collective_id=0, has_side_effects=True),
        )(x_t, g_t, wqkv_t, w_out, ln_gamma, ln_beta, temperature)

        nblk = tokens // BLK2
        tp_idx = lax.axis_index("tp").astype(jnp.int32).reshape(1)
        cols = pl.BlockSpec((D, BLK2), lambda i, st: (0, i))

        def whole(*shape):
            return pl.BlockSpec(shape, lambda i, st: (0,) * len(shape))

        y_t, dx_t, part = pl.pallas_call(
            rows_kernel,
            name="rows_kernel",
            out_shape=(sds((D, tokens), BF16), sds((D, tokens), BF16), sds((4, HD + 24, 256), F32)),
            grid_spec=pltpu.PrefetchScalarGridSpec(
                num_scalar_prefetch=1, grid=(nblk,),
                in_specs=[cols, cols, whole(4 * D, D), whole(4, D, D), whole(4, D, D), whole(4, D, 128)],
                out_specs=(cols, cols, whole(4, HD + 24, 256)),
                scratch_shapes=[pltpu.VMEM((4 * HD, D), F32), pltpu.VMEM((2, D, 128), F32),
                                pltpu.VMEM((4, D, SUB), BF16)]),
            compiler_params=pltpu.CompilerParams(dimension_semantics=("arbitrary",)),
        )(tp_idx, x_t, g_t, wt_full, w_full, mats, vecs)

        res = pl.pallas_call(
            reduce_kernel,
            name="reduce_kernel",
            out_shape=sds((HD + 24, 256), F32),
            in_specs=[vmem],
            out_specs=vmem,
            scratch_shapes=[pltpu.VMEM((4, HD + 24, 256), F32), dma((3,)), dma((3,))],
            compiler_params=pltpu.CompilerParams(collective_id=1, has_side_effects=True),
        )(part)
        gw, gwo, gg, gb, gt = pl.pallas_call(
            finish_kernel,
            name="finish_kernel",
            out_shape=(sds((3, HD, HD), F32), sds((12, D), F32), sds((D,), F32), sds((D,), F32), sds((NH,), F32)),
            in_specs=[vmem, vmem],
            out_specs=(vmem,) * 5,
        )(res, taus)
        return y_t.T, dx_t.T, jnp.transpose(gw, (1, 0, 2)), gwo, gg, gb, gt

    in_specs = (row_spec, row_spec, P(None, None, "tp"), P("tp", None), P(None), P(None), P(None))
    out_specs = (row_spec, row_spec, P(("dp", "sp"), None, "tp"), P(("dp", "tp", "sp"), None), P("dp"), P("dp"), P("dp"))
    return jax.shard_map(local_step, mesh=mesh, in_specs=in_specs, out_specs=out_specs, check_vma=False)
```

time: 947 us -> 70.3 us (0.07)
  waiting for transfers between devices: 791 us -> 0 us
  Pallas kernels: 0 us -> 69.1 us
  matrix products: 47.1 us -> 0 us
  other arithmetic: 41.9 us -> 0 us
  blocking collectives: 40.8 us -> 0 us
  between operations: 16.5 us -> 0.66 us
    psum x1 -> x0, waiting for transfers between devices: 791 us -> none  [local_step(): lax.psum(y_part, 'tp')]
    pallas_call x0 -> x4, Pallas kernels: none -> 69.1 us  [the longest x1 37.4 us: local_step(): pl.pallas_call(rows_kernel, name='rows_kernel', out_shape=(sds((D, tokens...]
    dot_general x11 -> x0, matrix products: 41.7 us -> none  [the longest x1 7.93 us: local_step(): jnp.einsum('nd,nec->dec', u_act, dqkv_act, preferred_element_type=jnp.flo...]
    unnamed x2 -> x0, blocking collectives: 20.5 us -> none
    psum x2 -> x0, blocking collectives: 20.2 us -> none  [the longest x1 13.5 us: local_step(): gram_mat, q_sq, k_sq = lax.psum((gram_part, q_part, k_part), 'sp')]
    reduce_sum x6 -> x0, other arithmetic: 19.9 us -> none  [the longest x1 11.2 us: local_step(): jnp.sum(grad_u * x_hat, axis=0)]
    convert_element_type x1 -> x0, other arithmetic: 15.5 us -> none  [local_step(): (grad_blk.astype(jnp.float32) + layer_norm_bwd(grad_u, x_hat, inv_std, ln...]
  transfers between devices with their start and end apart: 3 -> 0, of which waited for: 1 -> 0; matrix products, arithmetic and copies ran while one was open for 5% -> 0% of each run, Pallas kernels for 0% -> 0%
where the time goes in v1:
time: 70.3 us; the launch traced here: 69.8 us
  Pallas kernels  69.1 us (98%)
    pallas_call x1, Pallas kernels, local_step(): pl.pallas_call(rows_kernel, name='rows_kernel', out_shape=(sds((D, tokens...  37.4 us
    pallas_call x1, Pallas kernels, local_step(): pl.pallas_call(state_kernel, name='state_kernel', out_shape=(sds((4 * D,...  23.3 us
    pallas_call x1, Pallas kernels, local_step(): pl.pallas_call(reduce_kernel, name='reduce_kernel', out_shape=sds((HD + 2...  6.81 us
    pallas_call x1, Pallas kernels, local_step(): pl.pallas_call(finish_kernel, name='finish_kernel', out_shape=(sds((3, HD...  1.62 us

profile of v1, /device:TPU:0, one launch (start us, length us, event | category | flops | bytes accessed | tf_op | source)
XLA Modules:
  0.0 69.8 jit_solution(3017001025734676017)
XLA Ops:
  0.6 23.3 %state_kernel.1 = (bf16[768,192]{1,0:T(8,128)(2,1)}, bf16[4,192,192]{2,1,0:T(8,128)(2,1)}, bf16[4,192,192]{2,1,0:T(8,128)(2,1)}, f32[4,192,128]{2,1,0:T(8,128)}, f32[8,128]{1,0:T(8,128)}) custom-call(bf16[192,16384]{1,0:T(8,128)(2,1)} %bitcast.7, bf16[192,16384]{1,0:T(8,128)(2,1)} %bitcast.9, bf16[3,48,192]{2,1,0:T(8,128)(2,1)} %bitcast.11, ...), custom_call_target="tpu_custom_call" | custom-call | tf_op jit(solution)/shard_map/state_kernel/pallas_call | solution.py:317
  23.9 37.4 %rows_kernel.1 = (bf16[192,16384]{1,0:T(8,128)(2,1)}, bf16[192,16384]{1,0:T(8,128)(2,1)}, f32[4,72,256]{2,1,0:T(8,128)}) custom-call(s32[1]{0:T(128)} %bitcast.tp_ref, bf16[192,16384]{1,0:T(8,128)(2,1)} %bitcast.8, bf16[192,16384]{1,0:T(8,128)(2,1)} %bitcast.10, bf16[768,192]{1,0:T(8,128)(2,1)} %get-tuple-element.20.wt_ref, ...), custom_call_target="tpu_custom_call" | custom-call | tf_op jit(solution)/shard_map/rows_kernel/pallas_call | solution.py:343
  61.3 6.8 %reduce_kernel.1.res_ref = f32[72,256]{1,0:T(8,128)} custom-call(f32[4,72,256]{2,1,0:T(8,128)} %get-tuple-element.26.send_ref), custom_call_target="tpu_custom_call" | custom-call | tf_op jit(solution)/shard_map/reduce_kernel/pallas_call | solution.py:356
  68.2 1.6 %finish_kernel.1 = (f32[3,48,48]{2,1,0:T(8,128)}, f32[12,192]{1,0:T(8,128)}, f32[192]{0:T(256)}, f32[192]{0:T(256)}, f32[4]{0:T(128)}) custom-call(f32[72,256]{1,0:T(8,128)} %reduce_kernel.1.res_ref, f32[8,128]{1,0:T(8,128)} %get-tuple-element.27.tau_ref), custom_call_target="tpu_custom_call" | custom-call | tf_op jit(solution)/shard_map/finish_kernel/pallas_call | solution.py:365
